TPU v7x, 32 devices: a 4x2x2 block of a 4x4x8 slice. The times are simulated.
32 devices in a mesh: dp: 4 (over y, z), ep: 8 (over x, core).
Axes of the slice: x: 4, y: 2, z: 2, core: 2. Of those that a mesh axis runs over, the one named last changes fastest.
The devices are a block of a 4x4x8 slice.
Arguments:
- tokens: bfloat16 [6144, 2048], P(('dp', 'ep')), parts along dimension 0
- topk_idx: int32 [6144, 6], P(('dp', 'ep')), parts along dimension 0
- topk_w: float32 [6144, 6], P(('dp', 'ep')), parts along dimension 0
- w_up: bfloat16 [8, 9, 2048, 1408], P('ep')
- w_down: bfloat16 [8, 9, 1408, 2048], P('ep')
- slot_expert: int32 [8, 9], replicated
Outputs:
- output: bfloat16 [6144, 2048], P(('dp', 'ep')), parts along dimension 0
There are 4 independent parts. A program takes and returns all parts, laid end to end along the dimension named above; an argument that names none is the same for every part.
All inputs are finite; a program needn't handle non-finite values.
Results may differ from a plain program's by a relative error of at most 0.00137.
Values are sent between devices in bfloat16 or wider.
A program may use at most 768 MiB of HBM per device.

v0:
```python
import functools

import jax
import jax.numpy as jnp
from jax import lax
from jax.experimental import pallas as pl
from jax.experimental.pallas import tpu as pltpu
from jax.sharding import PartitionSpec as P

MESH = pl.DeviceIdType.MESH
F32 = jnp.float32
BF16 = jnp.bfloat16
LANES = 128
CHIPS = 4
AHEAD = 2
STAGES = 4
GROUP = 3
LAG = 3


def slot_bound(n_tok, n_top, n_dev, n_slot):
    base_load = (n_tok * n_top) // (n_dev * n_slot)
    return base_load + base_load // 2 + 1


def round_up(n, m):
    return -(-n // m) * m


def gelu(v):
    return v * (0.5 + 0.5 * jnp.tanh(v * (0.7978845608028654 + (0.7978845608028654 * 0.044715) * (v * v))))


def dot(a, b):
    return lax.dot_general(a, b, (((1,), (0,)), ((), ())), preferred_element_type=F32)


def moe_kernel(cfg, x_ref, idx_ref, gate_ref, tab_ref, wup_ref, wdn_ref, y_ref,
               xall, idx_all, gate_all, rank_all, tab, trk, g_buf, c_buf, xg, xg_odd, acc, h_buf, o_buf, o_odd, wu, wd, sib_in, far_in, sum_in, y_buf,
               in_s, meta_ss, meta_rs, out_ss, near_rs, rel_rs, sib_rs, wu_s, wd_s, ps_ss, ps_rs, pf_rs, fin_rs, y_s):
    bound, cap, kb_w, cb_w = (cfg[k] for k in ("bound", "cap", "kb_w", "cb_w"))
    odd = bound - cap
    n_tok, d_model = x_ref.shape
    n_top = idx_ref.shape[0]
    n_dev, n_slot = tab_ref.shape
    d_ff = wup_ref.shape[-1]
    d_main, d_mid = n_dev * cap, n_dev * bound
    rows_s = round_up(n_slot, 16)
    rows_main, rows_src = n_slot * cap, n_slot * cap + odd * rows_s
    n_kb, n_cb = d_model // kb_w, d_model // cb_w
    half = n_tok // 2
    me = lax.axis_index("ep")
    chip, core = me // 2, me % 2

    def dev(d_chip, d_core=0):
        return {"ep": ((chip + d_chip) % CHIPS) * 2 + (core + d_core) % 2}

    right, left, sib = dev(1), dev(CHIPS - 1), dev(0, 1)

    def rcopy(src, dst, ss, rs, to):
        return pltpu.make_async_remote_copy(src_ref=src, dst_ref=dst, send_sem=ss, recv_sem=rs, device_id=to, device_id_type=MESH)

    def took(ref, sem):
        rcopy(ref, ref, sem, sem, sib).wait_send()

    def arrived(ref, sem):
        rcopy(ref, ref, sem, sem, sib).wait_recv()

    groups = [(s, min(GROUP, n_slot - s)) for s in range(0, n_slot, GROUP)]

    class Loads:
        def __init__(self, src, dst, sem, g):
            (s, n), self.src, self.dst, self.sem = groups[g], src, dst, sem.at[g]
            self.slots, self.all = range(s, s + n), pl.ds(s, n)

        def start(self):
            for s in self.slots:
                pltpu.make_async_copy(self.src(s), self.dst.at[s], self.sem).start()

        def wait(self):
            pltpu.make_async_copy(self.src(self.all), self.dst.at[self.all], self.sem).wait()

    def up_load(kb, g):
        return Loads(lambda s: wup_ref.at[0, s, pl.ds(pl.multiple_of(kb * kb_w, kb_w), kb_w), :], wu, wu_s, g)

    def down_load(cb, g):
        return Loads(lambda s: wdn_ref.at[0, s, :, pl.ds(pl.multiple_of(cb * cb_w, cb_w), cb_w)], wd, wd_s, g)

    barrier = pltpu.get_barrier_semaphore()
    peers = [(1, 0), (2, 0), (CHIPS - 1, 0), (0, 1)]
    for dx, dc in peers:
        pl.semaphore_signal(barrier, inc=1, device_id=dev(dx, dc), device_id_type=MESH)
    in_meta = [pltpu.make_async_copy(idx_ref, idx_all.at[0], in_s.at[1]), pltpu.make_async_copy(gate_ref, gate_all.at[0], in_s.at[2]),
               pltpu.make_async_copy(tab_ref, tab, in_s.at[3])]
    for c in in_meta:
        c.start()
    for kb in range(n_kb):
        pltpu.make_async_copy(x_ref.at[:, pl.ds(kb * kb_w, kb_w)], xall.at[0, kb], in_s.at[0]).start()
    arrived(xall.at[0], in_s.at[0])
    for c in in_meta:
        c.wait()
    pl.semaphore_wait(barrier, len(peers))

    lo, hi = pl.ds(0, half), pl.ds(half, n_tok - half)
    prev = CHIPS - 1

    def near(kb):
        return (rcopy(xall.at[0, kb], xall.at[2 * prev, kb], out_ss.at[0], near_rs.at[kb], right),
                rcopy(xall.at[0, kb], xall.at[2, kb], out_ss.at[0], near_rs.at[kb], left))

    def relay(kb):
        return (rcopy(xall.at[2 * prev, kb, lo], xall.at[4, kb, lo], out_ss.at[1], rel_rs.at[kb], right),
                rcopy(xall.at[2, kb, hi], xall.at[4, kb, hi], out_ss.at[1], rel_rs.at[kb], left))

    def across(kb, off):
        return rcopy(xall.at[2 * off, kb], xall.at[2 * off + 1, kb], out_ss.at[2], sib_rs.at[kb], sib)

    def start_near(kb):
        for c in near(kb):
            c.start()

    def stage_near(kb):
        arrived(xall.at[pl.ds(0, 2), kb], near_rs.at[kb])
        for c in relay(kb):
            c.start()
        for off in (prev, 1):
            across(kb, off).start()

    def stage_far(kb):
        arrived(xall.at[4, kb], rel_rs.at[kb])
        across(kb, 2).start()

    def send_meta(ref, n):
        for dx in range(1, CHIPS):
            rcopy(ref.at[0], ref.at[2 * (CHIPS - dx)], meta_ss.at[n], meta_rs.at[n, 0], dev(dx)).start()
        rcopy(ref.at[0], ref.at[1], meta_ss.at[n], meta_rs.at[n, 1], sib).start()

    def hand_meta(ref, n):
        arrived(ref.at[pl.ds(0, CHIPS - 1)], meta_rs.at[n, 0])
        for off in range(1, CHIPS):
            rcopy(ref.at[2 * off], ref.at[2 * off + 1], meta_ss.at[n], meta_rs.at[n, 1], sib).start()

    def wait_meta(ref, n):
        arrived(ref.at[pl.ds(0, CHIPS)], meta_rs.at[n, 1])

    start_near(0)
    send_meta(idx_all, 0)
    for kb in range(1, AHEAD):
        start_near(kb)
    for kb in range(n_kb):
        across(kb, 0).start()
    for g in range(len(groups)):
        up_load(0, g).start()
    for g in range(len(groups)):
        down_load(0, g).start()

    sub = lax.broadcasted_iota(jnp.int32, (rows_s, n_slot), 0)
    lane = lax.broadcasted_iota(jnp.int32, (rows_s, n_slot), 1)
    my_row = tab[pl.ds(me, 1), :].astype(F32)
    e_col = jnp.sum(jnp.where(sub == lane, my_row, 0.0), axis=1, keepdims=True)
    e_col = jnp.where(sub[:, 0:1] < n_slot, e_col, -2.0)
    total = jnp.zeros((rows_s, n_slot), F32)
    before = jnp.zeros((rows_s, n_slot), F32)
    for d in range(n_dev):
        same = jnp.where(tab[d:d + 1, :].astype(F32) == e_col, 1.0, 0.0)
        total = total + same
        before = before + same * jnp.where(d < me, 1.0, 0.0)
    copies = jnp.sum(total, axis=1, keepdims=True)
    my_rank = jnp.sum(before, axis=1, keepdims=True)
    r = lax.broadcasted_iota(jnp.int32, (cap, LANES), 0)
    for s in range(n_slot):
        want = r.astype(F32) * copies[s:s + 1, :] + my_rank[s:s + 1, :]
        trk[s * cap:(s + 1) * cap, :] = want
    o_odd[...] = jnp.zeros_like(o_odd)

    def clear(q, carry):
        acc[q] = jnp.zeros(acc.shape[1:], F32)
        return carry

    lax.fori_loop(0, acc.shape[0], clear, 0)
    stage_near(0)
    start_near(AHEAD)
    hand_meta(idx_all, 0)
    wait_meta(idx_all, 0)
    earlier = (lax.broadcasted_iota(jnp.int32, (n_tok, n_tok), 0)
               < lax.broadcasted_iota(jnp.int32, (n_tok, n_tok), 1)).astype(F32).astype(BF16)
    rows_pad = round_up(rows_src, LANES)

    def hits(rank):
        for s in range(n_slot):
            yield s * cap, cap, rank[s:s + 1, :] == trk[s * cap:(s + 1) * cap, 0:1]
        for n in range(odd):
            yield rows_main + n * rows_s, rows_s, rank == float(cap + n) * copies + my_rank

    def route(j, carry):
        idx = idx_all[j].astype(F32)
        has = jnp.zeros((rows_s, n_tok), F32)
        for q in range(n_top):
            has = jnp.where(idx[q:q + 1, :] == e_col, 1.0, has)
        rank = jnp.where(has > 0.0, dot(has.astype(BF16), earlier), -1.0)
        rank_all[j] = rank
        for first, n, hit in hits(rank):
            g_buf[j, first:first + n, :] = jnp.where(hit, 1.0, 0.0).astype(BF16)
        return carry

    def route_gates(j):
        idx = idx_all[j].astype(F32)
        gates = gate_all[j]
        gate = jnp.zeros((rows_s, n_tok), F32)
        for q in range(n_top):
            gate = jnp.where(idx[q:q + 1, :] == e_col, gates[q:q + 1, :], gate)
        parts = []
        for first, n, hit in hits(rank_all[j]):
            s = first // cap
            parts.append(jnp.where(hit, gate[s:s + 1, :] if first < rows_main else gate, 0.0))
        if rows_pad > rows_src:
            parts.append(jnp.zeros((rows_pad - rows_src, n_tok), F32))
        left_over = jnp.transpose(jnp.concatenate(parts, axis=0))[:, :rows_src]
        for n in range(3):
            term = left_over.astype(BF16)
            c_buf[j, n * n_tok:(n + 1) * n_tok, :] = term
            left_over = left_over - term.astype(F32)

    lax.fori_loop(0, n_dev, route, 0)
    stage_near(1)
    start_near(AHEAD + 1)
    send_meta(gate_all, 1)
    route_gates(0)
    stage_far(0)

    chunks = [(n, min(2 * LANES, d_ff - n)) for n in range(0, d_ff, 2 * LANES)]
    n_mid = d_ff // LANES

    def up_block(kb, last, after):
        arrived(xall.at[pl.ds(0, CHIPS), kb], sib_rs.at[kb])

        for j in range(n_dev):
            rows = dot(g_buf[j], xall[j, kb])
            main = rows[:rows_main].astype(BF16)
            for s in range(n_slot):
                xg[s, j * cap:(j + 1) * cap, :] = main[s * cap:(s + 1) * cap]
            for n in range(odd):
                first = rows_main + n * rows_s
                for h in range(kb_w // LANES):
                    xg_odd[n, h, pl.ds(j, rows_s, stride=n_dev), :] = rows[first:first + rows_s, h * LANES:(h + 1) * LANES]
        for n in range(odd):
            for h in range(kb_w // LANES):
                for s in range(n_slot):
                    xg[s, d_main + n * n_dev:d_main + (n + 1) * n_dev, h * LANES:(h + 1) * LANES] = (
                        xg_odd[n, h, s * n_dev:(s + 1) * n_dev, :].astype(BF16))
        for g, (s0, n_s) in enumerate(groups):
            up_load(kb, g).wait()
            for s in range(s0, s0 + n_s):
                for n0, nw in chunks:
                    v = dot(xg[s], wu[s, :, n0:n0 + nw])
                    for n in range(0, nw, LANES):
                        q = s * n_mid + (n0 + n) // LANES
                        part = acc[q, :d_mid, :] + v[:, n:n + LANES]
                        if last:
                            h_buf[s, :, n0 + n:n0 + n + LANES] = gelu(part).astype(BF16)
                        else:
                            acc[q, :d_mid, :] = part
            if not last:
                up_load(kb + 1, g).start()
            if g in after:
                after[g]()

    def up_step(kb, carry):
        def near_2():
            @pl.when(kb + 2 < n_kb)
            def _():
                stage_near(kb + 2)

            @pl.when(kb + 2 + AHEAD < n_kb)
            def _():
                start_near(kb + 2 + AHEAD)

        def gates():
            @pl.when(kb == 1)
            def _():
                hand_meta(gate_all, 1)

            @pl.when(kb == 2)
            def _():
                wait_meta(gate_all, 1)

            @pl.when((kb >= 2) & (kb < 2 + n_dev // 2))
            def _():
                route_gates(2 * (kb - 2) + 1)
                route_gates(jnp.minimum(2 * (kb - 2) + 2, n_dev - 1))

        up_block(kb, False, {0: near_2, 1: lambda: stage_far(kb + 1), 2: gates})
        return carry

    assert n_kb - 1 >= 2 + n_dev // 2
    lax.fori_loop(0, n_kb - 1, up_step, 0)
    up_block(n_kb - 1, True, {})

    def mine(cb, off, h):
        return (cb * CHIPS + off) * 2 + h

    def staged(cb, off, h):
        return n_cb * CHIPS * 2 + ((cb % STAGES) * CHIPS + off) * 2 + h

    tok = pl.ds(0, n_tok)

    lots = {2: 0, 1: 1, prev: 1, 0: 2}

    def to_sib(cb, off):
        return rcopy(acc.at[pl.ds(staged(cb, off, 0), 2), tok], sib_in.at[cb, off], ps_ss.at[cb % STAGES], ps_rs.at[cb % 2, lots[off]], sib)

    def to_far(cb):
        return (rcopy(acc.at[mine(cb, 2, 0), tok], far_in.at[cb, 0], out_ss.at[3], pf_rs.at[cb], right),
                rcopy(acc.at[mine(cb, 2, 1), tok], far_in.at[cb, 1], out_ss.at[3], pf_rs.at[cb], left))

    def to_dir(cb):
        return (rcopy(acc.at[mine(cb, 1, 1), tok], sum_in.at[cb, 2], out_ss.at[4], fin_rs.at[cb], right),
                rcopy(acc.at[mine(cb, prev, 0), tok], sum_in.at[cb, 3], out_ss.at[4], fin_rs.at[cb], left))

    def to_mrg(cb):
        return (rcopy(far_in.at[cb, 0], sum_in.at[cb, 0], out_ss.at[5], fin_rs.at[cb], right),
                rcopy(far_in.at[cb, 1], sum_in.at[cb, 1], out_ss.at[5], fin_rs.at[cb], left))

    def merge(cb):
        arrived(far_in.at[cb], pf_rs.at[cb])
        for h, off in ((0, 1), (1, prev)):
            far_in[cb, h] = far_in[cb, h] + acc[mine(cb, off, h), :n_tok, :]
            to_mrg(cb)[h].start()

    def y_copy(cb):
        columns = pl.ds(pl.multiple_of(cb * cb_w, cb_w), cb_w)
        return pltpu.make_async_copy(y_buf.at[cb], y_ref.at[:, columns], y_s.at[cb])

    def finish(cb):
        arrived(sum_in.at[cb], fin_rs.at[cb])
        for h in range(2):
            out = acc[mine(cb, 0, h), :n_tok, :] + sum_in[cb, h] + sum_in[cb, 3 - h]
            y_buf[cb, :, h * LANES:(h + 1) * LANES] = out.astype(BF16)
        y_copy(cb).start()

    def add_sib(cb, off):
        for h in range(2):
            q = mine(cb, off, h)
            acc[q, :n_tok, :] = acc[q, :n_tok, :] + sib_in[cb, off, h]

    def combine(j, q):
        v = dot(c_buf[j], o_buf[j])
        v = (v[2 * n_tok:] + v[n_tok:2 * n_tok]) + v[:n_tok]
        for h in range(2):
            acc[q + h, :n_tok, :] = v[:, h * LANES:(h + 1) * LANES]

    def down_step(cb, carry):
        for g in range(len(groups)):
            down_load(cb, g).wait()
        for g, (s0, n_s) in enumerate(groups):
            for s in range(s0, s0 + n_s):
                out = dot(h_buf[s], wd[s])
                main = out[:d_main].astype(BF16)
                for j in range(n_dev):
                    o_buf[j, s * cap:(s + 1) * cap, :] = main[j * cap:(j + 1) * cap]
                for n in range(odd):
                    first = d_main + n * n_dev
                    for h in range(cb_w // LANES):
                        o_odd[n, h, pl.ds(s, n_dev, stride=rows_s), :] = out[first:first + n_dev, h * LANES:(h + 1) * LANES]


        for n in range(odd):
            first = rows_main + n * rows_s
            for h in range(cb_w // LANES):
                for j in range(n_dev):
                    o_buf[j, first:first + rows_s, h * LANES:(h + 1) * LANES] = o_odd[n, h, j * rows_s:(j + 1) * rows_s, :].astype(BF16)

        @pl.when(cb >= STAGES)
        def _():
            took(acc.at[pl.ds(staged(cb, 0, 0), 2 * CHIPS), tok], ps_ss.at[cb % STAGES])

        @pl.when(cb + 1 < n_cb)
        def _():
            for g in range(len(groups)):
                down_load(cb + 1, g).start()

        @pl.when(cb == 1)
        def _():
            merge(cb - 1)

        def for_sib(off):
            combine(2 * off + 1, staged(cb, off, 0))
            to_sib(cb, off).start()

        for off in (2, 1, prev):
            for_sib(off)
        combine(2 * 2, mine(cb, 2, 0))
        arrived(sib_in.at[cb, 2], ps_rs.at[cb % 2, 0])
        add_sib(cb, 2)
        for c in to_far(cb):
            c.start()
        for_sib(0)
        for off in (1, prev):
            combine(2 * off, mine(cb, off, 0))
        arrived(sib_in.at[cb, pl.ds(0, 2)], ps_rs.at[cb % 2, 1])
        for n, off in enumerate((1, prev)):
            add_sib(cb, off)
            to_dir(cb)[n].start()
        combine(0, mine(cb, 0, 0))

        @pl.when(cb >= LAG)
        def _():
            finish(cb - LAG)

        arrived(sib_in.at[cb, 0], ps_rs.at[cb % 2, 2])
        add_sib(cb, 0)

        @pl.when(cb >= 2)
        def _():
            merge(cb - 1)
        return carry

    lax.fori_loop(0, n_cb, down_step, 0)
    merge(n_cb - 1)
    for cb in range(max(0, n_cb - LAG), n_cb):
        finish(cb)

    others = pl.ds(1, n_dev - 1)
    took(idx_all.at[others], meta_ss.at[0])
    took(gate_all.at[others], meta_ss.at[1])
    for n, ref in enumerate((xall.at[pl.ds(0, 2)], xall.at[4], xall.at[pl.ds(0, CHIPS)], far_in, far_in, far_in)):
        took(ref, out_ss.at[n])
    for n in range(min(STAGES, n_cb)):
        took(acc.at[pl.ds(staged(n, 0, 0), 2 * CHIPS), tok], ps_ss.at[n])
    for cb in range(n_cb):
        y_copy(cb).wait()


def solution(mesh):
    assert mesh.shape["ep"] == 2 * CHIPS

    def group_layer(tokens, topk_idx, topk_w, w_up, w_down, slot_expert):
        n_tok, d_model = tokens.shape
        n_top = topk_idx.shape[1]
        n_dev, n_slot = slot_expert.shape
        d_ff = w_up.shape[-1]
        bound = slot_bound(n_tok, n_top, n_dev, n_slot)
        cap = bound // 8 * 8
        odd, rows_s = bound - cap, round_up(n_slot, 16)
        kb_w, cb_w = 2 * LANES, 2 * LANES
        n_kb, n_cb = d_model // kb_w, d_model // cb_w
        d_mid = n_dev * bound
        rows_src = n_slot * cap + odd * rows_s
        n_acc = max(n_slot * (d_ff // LANES), (n_cb + STAGES) * CHIPS * 2)
        cfg = dict(bound=bound, cap=cap, kb_w=kb_w, cb_w=cb_w)
        dma = pltpu.SemaphoreType.DMA
        hbm = pl.BlockSpec(memory_space=pl.ANY)
        return pl.pallas_call(
            functools.partial(moe_kernel, cfg),
            out_shape=jax.ShapeDtypeStruct((n_tok, d_model), BF16),
            in_specs=[hbm] * 6,
            out_specs=hbm,
            scratch_shapes=[
                pltpu.VMEM((n_dev, n_kb, n_tok, kb_w), BF16),
                pltpu.VMEM((n_dev, n_top, n_tok), jnp.int32),
                pltpu.VMEM((n_dev, n_top, n_tok), F32),
                pltpu.VMEM((n_dev, rows_s, n_tok), F32),
                pltpu.VMEM((n_dev, n_slot), jnp.int32),
                pltpu.VMEM((n_slot * cap, LANES), F32),
                pltpu.VMEM((n_dev, rows_src, n_tok), BF16),
                pltpu.VMEM((n_dev, 3 * n_tok, rows_src), BF16),
                pltpu.VMEM((n_slot, d_mid, kb_w), BF16),
                pltpu.VMEM((odd, kb_w // LANES, rows_s * n_dev, LANES), F32),
                pltpu.VMEM((n_acc, max(d_mid, n_tok), LANES), F32),
                pltpu.VMEM((n_slot, d_mid, d_ff), BF16),
                pltpu.VMEM((n_dev, rows_src, cb_w), BF16),
                pltpu.VMEM((odd, cb_w // LANES, n_dev * rows_s, LANES), F32),
                pltpu.VMEM((n_slot, kb_w, d_ff), BF16),
                pltpu.VMEM((n_slot, d_ff, cb_w), BF16),
                pltpu.VMEM((n_cb, CHIPS, 2, n_tok, LANES), F32),
                pltpu.VMEM((n_cb, 2, n_tok, LANES), F32),
                pltpu.VMEM((n_cb, 4, n_tok, LANES), F32),
                pltpu.VMEM((n_cb, n_tok, cb_w), BF16),
                dma((4,)), dma((2,)), dma((2, 2)), dma((6,)),
                dma((n_kb,)), dma((n_kb,)), dma((n_kb,)),
                dma((-(-n_slot // GROUP),)), dma((-(-n_slot // GROUP),)),
                dma((STAGES,)), dma((2, 3)), dma((n_cb,)), dma((n_cb,)), dma((n_cb,)),
            ],
            compiler_params=pltpu.CompilerParams(collective_id=0, has_side_effects=True, vmem_limit_bytes=67_000_000),
        )(tokens, topk_idx.T, topk_w.T, slot_expert, w_up, w_down)

    row_spec = P(('dp', 'ep'), None)
    weight_spec = P('ep', None, None, None)
    return jax.shard_map(group_layer, mesh=mesh, in_specs=(row_spec, row_spec, row_spec, weight_spec, weight_spec, P(None, None)),
                         out_specs=row_spec, check_vma=False)
```

profile of v0, /device:TPU:81, one launch (start us, length us, event | category | flops | bytes accessed | tf_op | source)
XLA Modules:
  0.0 102.0 jit_solution(9386177850850692463)
XLA Ops:
  0.0 99.9 %shard_map.64 = bf16[192,2048]{1,0:T(8,128)(2,1)} custom-call(bf16[192,2048]{1,0:T(8,128)(2,1)} %x_ref.1, s32[6,192]{1,0:T(8,128)} %bitcast.2, f32[6,192]{1,0:T(8,128)} %bitcast.3, s32[8,9]{1,0:T(8,128)} %tab_ref.1, bf16[1,9,2048,1408]{3,2,1,0:T(8,128)(2,1)} %wup_ref.1, bf16[1,9,1408,2048]{3,2,1,0:T(8,128)(2,1)} %wdn_ref.1), custom_call_target="tpu_custom_call" | custom-call | tf_op jit(solution)/shard_map/pallas_call | solution.py:453
  99.9 2.1 %copy.8 = bf16[192,2048]{1,0:T(8,128)(2,1)} copy(bf16[192,2048]{1,0:T(8,128)(2,1)} %shard_map.64) | data formatting | bytes 1572864
where the time goes:
time: 102 us
  Pallas kernels  99.9 us (98%)
  local copies, waits for them, and re-layouts  2.09 us (2%)
    pallas_call x1, Pallas kernels, group_layer(): pl.pallas_call(functools.partial(moe_kernel, cfg), out_shape=jax.ShapeDty...  99.9 us
    unnamed x1, local copies, waits for them, and re-layouts  2.09 us

commit v1 on v0

--- a/solution.py
+++ b/solution.py
@@ -335,7 +335,7 @@
         arrived(sum_in.at[cb], fin_rs.at[cb])
         for h in range(2):
             out = acc[mine(cb, 0, h), :n_tok, :] + sum_in[cb, h] + sum_in[cb, 3 - h]
-            y_buf[cb, :, h * LANES:(h + 1) * LANES] = out.astype(BF16)
+            y_buf[cb, :, h * LANES:(h + 1) * LANES] = out
         y_copy(cb).start()
 
     def add_sib(cb, off):
@@ -452,7 +452,7 @@
         hbm = pl.BlockSpec(memory_space=pl.ANY)
         return pl.pallas_call(
             functools.partial(moe_kernel, cfg),
-            out_shape=jax.ShapeDtypeStruct((n_tok, d_model), BF16),
+            out_shape=jax.ShapeDtypeStruct((n_tok, d_model), F32),
             in_specs=[hbm] * 6,
             out_specs=hbm,
             scratch_shapes=[
@@ -475,14 +475,14 @@
                 pltpu.VMEM((n_cb, CHIPS, 2, n_tok, LANES), F32),
                 pltpu.VMEM((n_cb, 2, n_tok, LANES), F32),
                 pltpu.VMEM((n_cb, 4, n_tok, LANES), F32),
-                pltpu.VMEM((n_cb, n_tok, cb_w), BF16),
+                pltpu.VMEM((n_cb, n_tok, cb_w), F32),
                 dma((4,)), dma((2,)), dma((2, 2)), dma((6,)),
                 dma((n_kb,)), dma((n_kb,)), dma((n_kb,)),
                 dma((-(-n_slot // GROUP),)), dma((-(-n_slot // GROUP),)),
                 dma((STAGES,)), dma((2, 3)), dma((n_cb,)), dma((n_cb,)), dma((n_cb,)),
             ],
             compiler_params=pltpu.CompilerParams(collective_id=0, has_side_effects=True, vmem_limit_bytes=67_000_000),
-        )(tokens, topk_idx.T, topk_w.T, slot_expert, w_up, w_down)
+        )(tokens, topk_idx.T, topk_w.T, slot_expert, w_up, w_down).astype(BF16)
 
     row_spec = P(('dp', 'ep'), None)
     weight_spec = P('ep', None, None, None)

time: 102 us -> 103 us (level)
  other arithmetic: 0 us -> 2.4 us
  local copies, waits for them, and re-layouts: 2.09 us -> 0 us
    convert_element_type x0 -> x1, other arithmetic: none -> 2.4 us  [group_layer(): return pl.pallas_call(functools.partial(moe_kernel, cfg), out_shape=jax.S...]
    unnamed x1 -> x0, local copies, waits for them, and re-layouts: 2.09 us -> none
where the time goes in v1:
time: 103 us; the launch traced here: 102 us
  Pallas kernels  100 us (97%)
  other arithmetic  2.4 us (2%)
    pallas_call x1, Pallas kernels, group_layer(): pl.pallas_call(functools.partial(moe_kernel, cfg), out_shape=jax.ShapeDty...  100 us
    convert_element_type x1, other arithmetic, group_layer(): return pl.pallas_call(functools.partial(moe_kernel, cfg), out_shape=jax.S...  2.4 us

profile of v1, /device:TPU:81, one launch (start us, length us, event | category | flops | bytes accessed | tf_op | source)
XLA Modules:
  0.0 102.4 jit_solution(3714559154312978328)
XLA Ops:
  0.0 100.0 %shard_map.64 = f32[192,2048]{1,0:T(8,128)} custom-call(bf16[192,2048]{1,0:T(8,128)(2,1)} %x_ref.1, s32[6,192]{1,0:T(8,128)} %bitcast.2, f32[6,192]{1,0:T(8,128)} %bitcast.3, s32[8,9]{1,0:T(8,128)} %tab_ref.1, bf16[1,9,2048,1408]{3,2,1,0:T(8,128)(2,1)} %wup_ref.1, bf16[1,9,1408,2048]{3,2,1,0:T(8,128)(2,1)} %wdn_ref.1), custom_call_target="tpu_custom_call" | custom-call | tf_op jit(solution)/shard_map/pallas_call | solution.py:453
  100.0 2.4 %convert_element_type.3 = bf16[192,2048]{1,0:T(8,128)(2,1)} convert(f32[192,2048]{1,0:T(8,128)} %shard_map.64) | non-fusion elementwise | flops 393216 | bytes 2359296 | tf_op jit(solution)/shard_map/convert_element_type | solution.py:485
